TPU v7x, 32 devices: a whole 2x2x4 slice. The times are simulated.
32 devices in a mesh: tm: 8 (over z, y), coef: 4 (over x, core).
Axes of the slice: x: 2, y: 2, z: 4, core: 2. Of those that a mesh axis runs over, the one named last changes fastest.
Arguments:
- design: bfloat16 [2048, 50176], P('tm', 'coef'), may hold values from -0.0390625 to 0.0390625
- observed: float32 [2048, 128], P('tm'), may hold values from -6 to 6
- slab_counts: int32 [8], P('tm'), may hold values from 128 to 256, as said below
- gap_mask: int32 [2048], P('tm'), may hold values 0 or 1
- filter_taps: float32 [128], replicated, may hold values from -0.5 to 1.2, as said below
- kaula_diag: float32 [50176], P('coef'), may hold values from 0.1 to 1
- precond: float32 [50176], P('coef'), may hold values from 0.3 to 3
Outputs:
- solution: float32 [50176, 128], P(('coef', 'tm'))
- residual: float32 [50176, 128], P(('coef', 'tm'))
Inputs may be any that keep to these rules, and one draw needn't show every extreme that they name: `slab_counts`: every slab holds at most 256 valid epochs, and some slab holds exactly 256. filter_taps[0] lies between 1 and 1.2.
All inputs are finite; a program needn't handle non-finite values. No bound on the sum of `gap_mask` on one device may be relied on, other than what follows from the above.
Results may differ from a plain program's by a relative error of at most 0.0065.
The roundings to bfloat16 on the way count: a program that leaves them out, or rounds other values in their place, can miss the bound.
Values may be sent and summed in bfloat16 or wider, within the bound.
No kernel may reach another device: no remote copies, remote signals or barrier semaphores. Data moves between devices by JAX's collectives and lax.ppermute only.
A program may use at most 64 MiB of HBM per device.

v0:
```python
import jax
import jax.numpy as jnp
from jax import lax
from jax.sharding import PartitionSpec as P

ITERS = 2
LANES = 128
BOTH = ("tm", "coef")


def toeplitz(pattern, band_len):
    tiled = jnp.tile(pattern, band_len)[: band_len * (2 * band_len - 1)]
    return tiled.reshape(band_len, 2 * band_len - 1)[:, :band_len]


def block_pair(filter_taps):
    band_len = filter_taps.shape[0]
    spacer = jnp.zeros((band_len,), jnp.float32)
    reversed_taps = filter_taps[:0:-1]
    lower = jnp.concatenate([filter_taps[:1], spacer, reversed_taps])
    upper = jnp.concatenate([jnp.zeros((1,), jnp.float32), reversed_taps, spacer])
    return (toeplitz(lower, band_len), toeplitz(upper, band_len))


def forward(values, lower_block, upper_block):
    band_len = lower_block.shape[0]
    blocks = values.reshape(-1, band_len, values.shape[1])
    previous = jnp.concatenate([jnp.zeros_like(blocks[:1]), blocks[:-1]], 0)
    result = jnp.einsum("ij,bjr->bir", lower_block, blocks, precision=lax.Precision.HIGHEST)
    result = result + jnp.einsum(
        "ij,bjr->bir", upper_block, previous, precision=lax.Precision.HIGHEST
    )
    return result.reshape(values.shape)


def backward(values, lower_block, upper_block):
    band_len = lower_block.shape[0]
    blocks = values.reshape(-1, band_len, values.shape[1])
    following = jnp.concatenate([blocks[1:], jnp.zeros_like(blocks[:1])], 0)
    result = jnp.einsum("ji,bjr->bir", lower_block, blocks, precision=lax.Precision.HIGHEST)
    result = result + jnp.einsum(
        "ji,bjr->bir", upper_block, following, precision=lax.Precision.HIGHEST
    )
    return result.reshape(values.shape)


def shards(design, observed, slab_counts, gap_mask, filter_taps, kaula_diag, precond):
    epoch_rows, coef_rows = design.shape
    slabs = lax.axis_size("tm")
    owned_rows = coef_rows // slabs
    owner_index = lax.axis_index("tm")
    tile = LANES if coef_rows % LANES == 0 else owned_rows
    tiles = coef_rows // tile
    width = max(
        (-(-(slab + 1) * owned_rows // tile) - slab * owned_rows // tile for slab in range(slabs))
    )
    first_tiles = [min(slab * owned_rows // tile, tiles - width) for slab in range(slabs)]
    window = width * tile
    begins = [first * tile for first in first_tiles]
    begin = jnp.array(begins, jnp.int32)[owner_index]
    offset = owner_index * owned_rows - begin
    pieces = jnp.stack([design[:, start : start + window] for start in begins])
    columns = lax.all_to_all(pieces, "tm", 0, 0).reshape(slabs * epoch_rows, window)
    position = jnp.arange(epoch_rows, dtype=jnp.int32)
    own_weight = ((gap_mask == 1) & (position < slab_counts[0])).astype(jnp.float32)
    packed = jnp.concatenate(
        [observed, jnp.broadcast_to(own_weight[:, None], (epoch_rows, LANES))], 1
    )
    packed = lax.all_gather(packed, "tm", axis=0, tiled=True)
    observed_all = packed[:, : observed.shape[1]]
    weight = packed[:, observed.shape[1] : observed.shape[1] + 1]
    lower_block, upper_block = block_pair(filter_taps)

    def weighted(values):
        inner = forward(weight * values, lower_block, upper_block)
        return (weight * backward(inner, lower_block, upper_block)).astype(jnp.bfloat16)

    def transposed(filtered):
        return lax.dot_general(
            columns, filtered, (((0,), (0,)), ((), ())), preferred_element_type=jnp.float32
        )

    def reduced(vector, rows):
        product = jnp.dot(columns, vector.astype(jnp.bfloat16), preferred_element_type=jnp.float32)
        extra = jnp.stack(rows + [jnp.zeros_like(rows[0])] * (8 - len(rows)))
        total = lax.psum(jnp.concatenate([product, extra]), BOTH)
        return (total[: product.shape[0]], [total[product.shape[0] + i] for i in range(len(rows))])

    local = jnp.arange(window, dtype=jnp.int32)
    owned = (local >= offset) & (local < offset + owned_rows)

    def window_of(values):
        cut = lax.dynamic_slice_in_dim(values, begin, window, 0)
        return jnp.where(owned, cut, 0.0)[:, None]

    kaula_col = window_of(kaula_diag)
    precond_col = window_of(precond)
    residual = transposed(weighted(observed_all))
    solution = jnp.zeros_like(residual)
    direction = None
    for iteration in range(ITERS):
        scaled = precond_col * residual
        rows = [jnp.sum(residual * scaled, 0), jnp.sum(kaula_col * scaled * scaled, 0)]
        if iteration:
            rows.append(jnp.sum(kaula_col * scaled * direction, 0))
        product, sums = reduced(scaled, rows)
        if iteration:
            ratio = sums[0] / norm_now
            direction = scaled + ratio * direction
            slab_values = product + ratio * slab_values
            ridge = sums[1] + 2.0 * ratio * sums[2] + ratio * ratio * ridge
        else:
            direction, slab_values, ridge = (scaled, product, sums[1])
        norm_now = sums[0]
        filtered = weighted(slab_values)
        curvature = jnp.sum(slab_values * filtered.astype(jnp.float32), 0) + ridge
        image = transposed(filtered) + kaula_col * direction
        step_len = norm_now / curvature
        solution = solution + step_len * direction
        residual = residual - step_len * image
    return tuple(
        (lax.dynamic_slice_in_dim(values, offset, owned_rows, 0) for values in (solution, residual))
    )


def solution(mesh):
    placed = (P("tm", "coef"), P("tm", None), P("tm"), P("tm"), P(), P("coef"), P("coef"))
    return jax.shard_map(
        shards,
        mesh=mesh,
        in_specs=placed,
        out_specs=(P(("coef", "tm"), None), P(("coef", "tm"), None)),
        check_vma=False,
    )
```

profile of v0, /device:TPU:0, one launch (start us, length us, event | category | flops | bytes accessed | tf_op | source)
XLA Modules:
  0.0 519.3 jit_solution(8027475732928325640)
XLA Ops:
  7.2 0.0 copy-start.1
  7.2 2.3 bitcast_dynamic-update-slice_fusion.7
  9.5 2.3 bitcast_dynamic-update-slice_fusion.6
  11.7 2.2 bitcast_dynamic-update-slice_fusion.5
  13.9 2.1 bitcast_dynamic-update-slice_fusion.4
  16.1 1.0 bitcast_dynamic-update-slice_fusion.3
  17.0 1.0 bitcast_dynamic-update-slice_fusion.2
  18.0 1.0 bitcast_dynamic-update-slice_fusion.1
  19.0 1.0 bitcast_dynamic-update-slice_fusion
  20.1 7.5 %all-to-all-start = ((bf16[8,256,1664]{2,1,0:T(8,128)(2,1)}), bf16[8,256,1664]{2,1,0:T(8,128)(2,1)}, u32[]{:S(2)}, u32[]{:S(2)}) async-start(bf16[8,256,1664]{2,1,0:T(8,128)(2,1)} %bitcast_dynamic-update-slice_fusion), calls=%async_computation | async-start | bytes 13631488 | tf_op jit(solution)/shard_map/all_to_all | solution.py:63
  27.5 0.0 all-gather.2.cloned.1.call-start
  28.2 0.1 broadcast_in_dim.10
  28.3 0.7 pad_maximum_fusion
  29.1 0.0 all-gather.2.cloned.1.call-update
  29.1 0.0 all-reduce.9.cloned.1.call-start
  29.1 0.6 dynamic_slice.15
  31.7 0.1 slice.107
  31.8 0.1 rev.3
  31.9 0.1 pad_maximum_fusion.2
  32.0 0.1 copy.66
  32.1 0.3 reshape.59
  32.4 0.1 copy.67
  32.5 0.3 reshape.60
  33.5 0.8 dynamic-slice_select_fusion
  34.3 0.8 dynamic-slice_select_fusion.1
  35.1 140.5 %all-gather.2.cloned.1.call-done = f32[2048,256]{1,0:T(8,128)} async-done(((f32[256,256]{1,0:T(8,128)}), f32[2048,256]{1,0:T(8,128)}) %all-gather.2.cloned.1.call-update) | async-done | bytes 2097168 | tf_op jit(solution)/shard_map/all_gather | solution.py:69
  175.5 1.6 slice_reduce_fusion
  177.1 1.6 slice_multiply_fusion
  178.7 0.1 slice.132
  178.8 1.8 fusion.29
  180.6 1.7 fusion.4
  182.3 1.1 fusion.26
  183.4 1.1 fusion.6
  184.5 17.8 %all-to-all-done = bf16[8,256,1664]{2,1,0:T(8,128)(2,1)} async-done(((bf16[8,256,1664]{2,1,0:T(8,128)(2,1)}), bf16[8,256,1664]{2,1,0:T(8,128)(2,1)}, u32[]{:S(2)}, u32[]{:S(2)}) %all-to-all-start) | async-done | bytes 6815776 | tf_op jit(solution)/shard_map/all_to_all | solution.py:63
  202.3 5.3 %fusion.15 = (f32[128]{0:T(128)S(1)}, f32[128]{0:T(128)S(1)}, f32[1664,128]{1,0:T(8,128)S(1)}) fusion(f32[1664]{0:T(1024)S(1)} %dynamic-slice_select_fusion, f32[1664]{0:T(1024)S(1)} %dynamic-slice_select_fusion.1, bf16[2048,1664]{1,0:T(8,128)(2,1)} %bitcast.8, bf16[2048,128]{1,0:T(8,128)(2,1)S(1)} %bitcast.152), kind=kOutput, calls=%fused_computation.38 | convolution fusion | flops 873692928 | bytes 8206336 | tf_op jit(solution)/shard_map/dot_general | solution.py:79
  207.6 5.3 %fusion.20 = f32[2048,128]{1,0:T(8,128)S(1)} fusion(bf16[2048,1664]{1,0:T(8,128)(2,1)} %bitcast.8, f32[1664,128]{1,0:T(8,128)S(1)} %get-tuple-element.13, f32[1664]{0:T(1024)S(1)} %dynamic-slice_select_fusion.1), kind=kOutput, calls=%fused_computation.57 | convolution fusion | flops 872841216 | bytes 8722944 | tf_op jit(solution)/shard_map/dot_general | solution.py:84
  212.9 2.3 concatenate.42
  215.2 0.0 all-reduce.9.cloned.1.call-update
  215.2 0.2 all-reduce.11.cloned.1.call-start
  215.4 129.3 %all-reduce.9.cloned.1.call-done = f32[2056,128]{1,0:T(8,128)} async-done(((f32[2056,128]{1,0:T(8,128)}), f32[2056,128]{1,0:T(8,128)}) %all-reduce.9.cloned.1.call-update) | async-done | bytes 1052688 | tf_op jit(solution)/shard_map/psum | solution.py:86
  344.7 1.6 slice_multiply_fusion.1
  346.3 0.1 slice.138
  346.4 1.8 fusion.28
  348.2 1.7 fusion.3
  349.9 1.1 fusion.25
  351.0 1.2 fusion.10
  352.2 0.4 multiply_reduce_fusion.1
  352.5 5.4 %fusion.17 = (f32[128]{0:T(128)S(1)}, f32[128]{0:T(128)S(1)}, f32[128]{0:T(128)S(1)}, f32[1664,128]{1,0:T(8,128)S(1)}) fusion(f32[1664,128]{1,0:T(8,128)S(1)} %get-tuple-element.13, f32[1664]{0:T(1024)S(1)} %dynamic-slice_select_fusion, f32[1664]{0:T(1024)S(1)} %dynamic-slice_select_fusion.1, bf16[2048,1664]{1,0:T(8,128)(2,1)} %bitcast.8, ...), kind=kOutput, calls=%fused_computation.40 | convolution fusion | flops 875183744 | bytes 9059328 | tf_op jit(solution)/shard_map/dot_general | solution.py:79
  358.0 5.1 fusion.21
  363.0 2.5 concatenate.45
  365.5 0.0 all-reduce.11.cloned.1.call-update
  365.5 0.1 dynamic-slice
  365.6 130.8 %all-reduce.11.cloned.1.call-done = f32[2056,128]{1,0:T(8,128)} async-done(((f32[2056,128]{1,0:T(8,128)}), f32[2056,128]{1,0:T(8,128)}) %all-reduce.11.cloned.1.call-update) | async-done | bytes 1052688 | tf_op jit(solution)/shard_map/psum | solution.py:86
  496.4 0.7 slice_divide_fusion
  497.1 1.4 multiply_add_fusion
  498.6 1.6 broadcast_multiply_fusion
  500.1 0.1 slice.143
  500.2 1.8 fusion.27
  502.0 1.7 fusion.2
  503.7 1.1 fusion.24
  504.8 1.2 fusion.9
  506.0 4.9 fusion.37
  511.0 0.4 multiply_reduce_fusion
  511.3 1.5 dynamic-slice_subtract_fusion
  (23 shorter events, 0.1 us)
Async XLA Ops:
  7.2 8.9 %copy-start.1 = (bf16[256,12544]{1,0:T(8,128)(2,1)S(1)}, bf16[256,12544]{1,0:T(8,128)(2,1)}, u32[]{:S(2)}) copy-start(bf16[256,12544]{1,0:T(8,128)(2,1)} %param.8) | copy-start | bytes 19267588
  20.0 8.2 %copy-start.5 = (s32[256]{0:T(256)S(1)}, s32[256]{0:T(256)}, u32[]{:S(2)}) copy-start(s32[256]{0:T(256)} %param.11) | copy-start | bytes 3076
  20.0 8.3 %copy-start.4 = (f32[256,128]{1,0:T(8,128)S(1)}, f32[256,128]{1,0:T(8,128)}, u32[]{:S(2)}) copy-start(f32[256,128]{1,0:T(8,128)} %param.9) | copy-start | bytes 393220
  20.0 9.1 %copy-start.7 = (s32[8]{0:T(128)S(1)}, s32[8]{0:T(128)}, u32[]{:S(2)}) copy-start(s32[8]{0:T(128)} %constant.9.clone) | copy-start | bytes 100
  20.1 11.6 %copy-start.6 = (f32[128]{0:T(128)S(1)}, f32[128]{0:T(128)}, u32[]{:S(2)}) copy-start(f32[128]{0:T(128)} %param.12) | copy-start | bytes 1540
  20.1 182.2 %all-to-all-start = ((bf16[8,256,1664]{2,1,0:T(8,128)(2,1)}), bf16[8,256,1664]{2,1,0:T(8,128)(2,1)}, u32[]{:S(2)}, u32[]{:S(2)}) async-start(bf16[8,256,1664]{2,1,0:T(8,128)(2,1)} %bitcast_dynamic-update-slice_fusion), calls=%async_computation | async-start | bytes 13631488 | tf_op jit(solution)/shard_map/all_to_all | solution.py:63
  27.5 148.0 %all-gather.2.cloned.1.call-start = ((), (), s32[]{:S(2)}) async-start(), calls=%async_computation.1 | async-start | bytes 2359296 | tf_op jit(solution)/shard_map/all_gather | solution.py:69
  29.1 315.7 %all-reduce.9.cloned.1.call-start = ((), (), s32[]{:S(2)}) async-start(), calls=%async_computation.2 | async-start | bytes 2105344 | tf_op jit(solution)/shard_map/psum | solution.py:86
  207.6 145.0 %copy-start.3 = (f32[1664,128]{1,0:T(8,128)}, f32[1664,128]{1,0:T(8,128)S(1)}, u32[]{:S(2)}) copy-start(f32[1664,128]{1,0:T(8,128)S(1)} %get-tuple-element.13) | copy-start | bytes 2555908
  215.2 281.2 %all-reduce.11.cloned.1.call-start = ((), (), s32[]{:S(2)}) async-start(), calls=%async_computation.3 | async-start | bytes 2105344 | tf_op jit(solution)/shard_map/psum | solution.py:86
  346.3 5.9 %copy-start = (f32[2056,128]{1,0:T(8,128)S(1)}, f32[2056,128]{1,0:T(8,128)}, u32[]{:S(2)}) copy-start(f32[2056,128]{1,0:T(8,128)} %all-reduce.9.cloned.1.call-done) | copy-start | bytes 3158020
  504.8 6.1 %copy-start.2 = (f32[2056,128]{1,0:T(8,128)S(1)}, f32[2056,128]{1,0:T(8,128)}, u32[]{:S(2)}) copy-start(f32[2056,128]{1,0:T(8,128)} %all-reduce.11.cloned.1.call-done) | copy-start | bytes 3158020
Sparse Core Ops, SparseCore 0:
  31.0 144.4 all-gather.1
  215.3 129.3 all-reduce.8
  365.7 130.7 all-reduce.10
where the time goes:
time: 520 us; the launch traced here: 519 us
  waiting for transfers between devices  418 us (80%)
  matrix products  43.2 us (8%)
  local copies, waits for them, and re-layouts  21.2 us (4%)
  between operations  17.4 us (3%)
  other arithmetic  11.4 us (2%)
  starting transfers between devices  7.75 us (1%)
    psum x2, waiting for transfers between devices, reduced(): total = lax.psum(jnp.concatenate([product, extra]), BOTH)  260 us
    all_gather x1, waiting for transfers between devices, shards(): packed = lax.all_gather(packed, 'tm', axis=0, tiled=True)  140 us
    all_to_all x1, waiting for transfers between devices, shards(): lax.all_to_all(pieces, 'tm', 0, 0).reshape(slabs * epoch_rows, window)  17.8 us
    dot_general x3, matrix products, transposed(): lax.dot_general(columns, filtered, (((0,), (0,)), ((), ())), preferred_el...  15.7 us
    unnamed x26, local copies, waits for them, and re-layouts  12 us
  transfers between devices with their start and end apart: 4, of which 4 were waited for; matrix products, arithmetic and copies ran while one was open for 3% of the time, Pallas kernels for 0%

commit v1 on v0

--- a/solution.py
+++ b/solution.py
@@ -83,7 +83,7 @@
     def reduced(vector, rows):
         product = jnp.dot(columns, vector.astype(jnp.bfloat16), preferred_element_type=jnp.float32)
         extra = jnp.stack(rows + [jnp.zeros_like(rows[0])] * (8 - len(rows)))
-        total = lax.psum(jnp.concatenate([product, extra]), BOTH)
+        total = jnp.sum(lax.all_gather(jnp.concatenate([product, extra]), BOTH), axis=0)
         return (total[: product.shape[0]], [total[product.shape[0] + i] for i in range(len(rows))])
 
     local = jnp.arange(window, dtype=jnp.int32)

time: 520 us -> 668 us (1.28)
  waiting for transfers between devices: 418 us -> 545 us
  other arithmetic: 11.4 us -> 32.6 us
    all_gather x0 -> x2, waiting for transfers between devices: none -> 387 us  [reduced(): lax.all_gather(jnp.concatenate([product, extra]), BOTH)]
    psum x2 -> x0, waiting for transfers between devices: 260 us -> none  [reduced(): total = lax.psum(jnp.concatenate([product, extra]), BOTH)]
    reduce_sum x0 -> x2, other arithmetic: none -> 24.3 us  [reduced(): jnp.sum(lax.all_gather(jnp.concatenate([product, extra]), BOTH), axis=0)]
  transfers between devices with their start and end apart: 4 -> 4, of which waited for: 4 -> 4; matrix products, arithmetic and copies ran while one was open for 3% -> 2% of each run, Pallas kernels for 0% -> 0%
where the time goes in v1:
time: 668 us; the launch traced here: 667 us
  waiting for transfers between devices  545 us (82%)
  matrix products  43.2 us (6%)
  other arithmetic  32.6 us (5%)
  local copies, waits for them, and re-layouts  20.7 us (3%)
  between operations  17.3 us (3%)
  starting transfers between devices  7.75 us (1%)
    all_gather x2, waiting for transfers between devices, reduced(): lax.all_gather(jnp.concatenate([product, extra]), BOTH)  387 us
    all_gather x1, waiting for transfers between devices, shards(): packed = lax.all_gather(packed, 'tm', axis=0, tiled=True)  140 us
    reduce_sum x2, other arithmetic, reduced(): jnp.sum(lax.all_gather(jnp.concatenate([product, extra]), BOTH), axis=0)  24.3 us
    all_to_all x1, waiting for transfers between devices, shards(): lax.all_to_all(pieces, 'tm', 0, 0).reshape(slabs * epoch_rows, window)  17.8 us
    dot_general x3, matrix products, transposed(): lax.dot_general(columns, filtered, (((0,), (0,)), ((), ())), preferred_el...  15.7 us
  transfers between devices with their start and end apart: 4, of which 4 were waited for; matrix products, arithmetic and copies ran while one was open for 2% of the time, Pallas kernels for 0%

profile of v1, /device:TPU:0, one launch (start us, length us, event | category | flops | bytes accessed | tf_op | source)
XLA Modules:
  0.0 666.8 jit_solution(18249154300047697722)
XLA Ops:
  7.2 2.3 bitcast_dynamic-update-slice_fusion.7
  9.5 2.3 bitcast_dynamic-update-slice_fusion.6
  11.7 2.1 bitcast_dynamic-update-slice_fusion.5
  13.8 2.1 bitcast_dynamic-update-slice_fusion.4
  16.0 1.0 bitcast_dynamic-update-slice_fusion.3
  16.9 1.0 bitcast_dynamic-update-slice_fusion.2
  17.9 1.0 bitcast_dynamic-update-slice_fusion.1
  18.9 1.0 bitcast_dynamic-update-slice_fusion
  19.9 7.5 %all-to-all-start = ((bf16[8,256,1664]{2,1,0:T(8,128)(2,1)}), bf16[8,256,1664]{2,1,0:T(8,128)(2,1)}, u32[]{:S(2)}, u32[]{:S(2)}) async-start(bf16[8,256,1664]{2,1,0:T(8,128)(2,1)} %bitcast_dynamic-update-slice_fusion), calls=%async_computation | async-start | bytes 13631488 | tf_op jit(solution)/shard_map/all_to_all | solution.py:63
  27.4 0.0 all-gather.6.cloned.1.call-start
  28.1 0.1 broadcast_in_dim.10
  28.2 0.7 pad_maximum_fusion
  28.9 0.0 all-gather.6.cloned.1.call-update
  28.9 0.0 all-gather.8.cloned.1.call-start
  29.0 0.6 dynamic_slice.15
  31.5 0.1 slice.107
  31.6 0.1 rev.3
  31.7 0.1 pad_maximum_fusion.2
  31.8 0.1 copy.65
  31.9 0.3 reshape.60
  32.3 0.1 copy.64
  32.3 0.3 reshape.59
  33.3 0.8 dynamic-slice_select_fusion.1
  34.1 0.8 dynamic-slice_select_fusion
  34.9 140.5 %all-gather.6.cloned.1.call-done = f32[2048,256]{1,0:T(8,128)} async-done(((f32[256,256]{1,0:T(8,128)}), f32[2048,256]{1,0:T(8,128)}) %all-gather.6.cloned.1.call-update) | async-done | bytes 2097168 | tf_op jit(solution)/shard_map/all_gather | solution.py:69
  175.4 1.6 slice_reduce_fusion
  177.0 1.6 slice_multiply_fusion
  178.5 0.1 slice.132
  178.6 1.8 fusion.29
  180.4 1.7 fusion.4
  182.1 1.1 fusion.26
  183.2 1.1 fusion.6
  184.3 17.8 %all-to-all-done = bf16[8,256,1664]{2,1,0:T(8,128)(2,1)} async-done(((bf16[8,256,1664]{2,1,0:T(8,128)(2,1)}), bf16[8,256,1664]{2,1,0:T(8,128)(2,1)}, u32[]{:S(2)}, u32[]{:S(2)}) %all-to-all-start) | async-done | bytes 6815776 | tf_op jit(solution)/shard_map/all_to_all | solution.py:63
  202.1 5.3 fusion.15
  207.4 5.3 fusion.20
  212.7 2.2 concatenate.42
  215.0 0.0 all-gather.8.cloned.1.call-update
  215.0 0.2 all-gather.10.cloned.1.call-start
  215.2 193.8 %all-gather.8.cloned.1.call-done = f32[65792,128]{1,0:T(8,128)} async-done(((f32[2056,128]{1,0:T(8,128)}), f32[65792,128]{1,0:T(8,128)}) %all-gather.8.cloned.1.call-update) | async-done | bytes 33685520 | tf_op jit(solution)/shard_map/all_gather | solution.py:86
  409.0 12.0 %reduce_sum.87 = f32[2056,128]{1,0:T(8,128)S(1)} reduce(f32[32,2056,128]{2,1,0:T(8,128)} %bitcast.144, f32[]{:T(128)} %constant.4.clone.1), dimensions={0}, to_apply=%region_2.3 | reduce | flops 8158208 | bytes 34738180 | tf_op jit(solution)/shard_map/reduce_sum | solution.py:86
  421.0 0.3 slice_multiply_fusion.1
  421.3 0.1 slice.138
  421.4 1.8 fusion.28
  423.2 1.7 fusion.3
  424.9 1.1 fusion.25
  426.0 1.1 fusion.10
  427.2 0.4 multiply_reduce_fusion.1
  427.5 5.4 fusion.17
  432.9 5.1 fusion.21
  438.0 2.2 concatenate.45
  440.2 0.0 all-gather.10.cloned.1.call-update
  440.3 0.1 dynamic-slice
  440.3 193.1 %all-gather.10.cloned.1.call-done = f32[65792,128]{1,0:T(8,128)} async-done(((f32[2056,128]{1,0:T(8,128)}), f32[65792,128]{1,0:T(8,128)}) %all-gather.10.cloned.1.call-update) | async-done | bytes 33685520 | tf_op jit(solution)/shard_map/all_gather | solution.py:86
  633.5 12.3 %reduce_sum.93 = f32[2056,128]{1,0:T(8,128)S(1)} reduce(f32[32,2056,128]{2,1,0:T(8,128)} %bitcast.143, f32[]{:T(128)} %constant.4.clone.1), dimensions={0}, to_apply=%region_7.8 | reduce | flops 8158208 | bytes 34738180 | tf_op jit(solution)/shard_map/reduce_sum | solution.py:86
  645.8 1.4 multiply_add_fusion
  647.3 0.3 broadcast_multiply_fusion
  647.6 0.1 slice.143
  647.7 1.8 fusion.27
  649.5 1.7 fusion.2
  651.2 1.1 fusion.24
  652.3 1.2 fusion.9
  653.5 0.4 multiply_reduce_fusion
  653.9 4.9 fusion.37
  658.8 1.4 dynamic-slice_subtract_fusion
  (21 shorter events, 0.1 us)
Async XLA Ops:
  7.2 8.8 %copy-start = (bf16[256,12544]{1,0:T(8,128)(2,1)S(1)}, bf16[256,12544]{1,0:T(8,128)(2,1)}, u32[]{:S(2)}) copy-start(bf16[256,12544]{1,0:T(8,128)(2,1)} %param.8) | copy-start | bytes 19267588
  19.9 8.2 %copy-start.3 = (s32[256]{0:T(256)S(1)}, s32[256]{0:T(256)}, u32[]{:S(2)}) copy-start(s32[256]{0:T(256)} %param.11) | copy-start | bytes 3076
  19.9 8.3 %copy-start.2 = (f32[256,128]{1,0:T(8,128)S(1)}, f32[256,128]{1,0:T(8,128)}, u32[]{:S(2)}) copy-start(f32[256,128]{1,0:T(8,128)} %param.9) | copy-start | bytes 393220
  19.9 9.1 %copy-start.5 = (s32[8]{0:T(128)S(1)}, s32[8]{0:T(128)}, u32[]{:S(2)}) copy-start(s32[8]{0:T(128)} %constant.9.clone) | copy-start | bytes 100
  19.9 11.6 %copy-start.4 = (f32[128]{0:T(128)S(1)}, f32[128]{0:T(128)}, u32[]{:S(2)}) copy-start(f32[128]{0:T(128)} %param.12) | copy-start | bytes 1540
  19.9 182.2 %all-to-all-start = ((bf16[8,256,1664]{2,1,0:T(8,128)(2,1)}), bf16[8,256,1664]{2,1,0:T(8,128)(2,1)}, u32[]{:S(2)}, u32[]{:S(2)}) async-start(bf16[8,256,1664]{2,1,0:T(8,128)(2,1)} %bitcast_dynamic-update-slice_fusion), calls=%async_computation | async-start | bytes 13631488 | tf_op jit(solution)/shard_map/all_to_all | solution.py:63
  27.4 148.0 %all-gather.6.cloned.1.call-start = ((), (), s32[]{:S(2)}) async-start(), calls=%async_computation.1 | async-start | bytes 2359296 | tf_op jit(solution)/shard_map/all_gather | solution.py:69
  28.9 380.1 %all-gather.8.cloned.1.call-start = ((), (), s32[]{:S(2)}) async-start(), calls=%async_computation.2 | async-start | bytes 34738176 | tf_op jit(solution)/shard_map/all_gather | solution.py:86
  207.4 220.1 %copy-start.1 = (f32[1664,128]{1,0:T(8,128)}, f32[1664,128]{1,0:T(8,128)S(1)}, u32[]{:S(2)}) copy-start(f32[1664,128]{1,0:T(8,128)S(1)} %get-tuple-element.13) | copy-start | bytes 2555908
  215.0 418.5 %all-gather.10.cloned.1.call-start = ((), (), s32[]{:S(2)}) async-start(), calls=%async_computation.3 | async-start | bytes 34738176 | tf_op jit(solution)/shard_map/all_gather | solution.py:86
Sparse Core Ops, SparseCore 0:
  30.9 144.4 all-gather.5
  215.1 193.8 all-gather.7
  440.4 193.0 all-gather.9
